TPU v7x, 32 devices: a whole 2x2x4 slice. The times are simulated.
32 devices in a mesh: seq: 8 (over z, y), head: 4 (over x, core).
Axes of the slice: x: 2, y: 2, z: 4, core: 2. Of those that a mesh axis runs over, the one named last changes fastest.
Arguments:
- query: bfloat16 [8, 40, 128], P(None, 'head'), may hold values from -400 to 400
- key_cache: bfloat16 [8, 4096, 8, 128], P(None, 'seq', 'head'), may hold values from -6 to 6
- value_cache: bfloat16 [8, 4096, 8, 128], P(None, 'seq', 'head'), may hold values from -6 to 6
- new_key: bfloat16 [8, 8, 128], P(None, 'head'), may hold values from -6 to 6
- new_value: bfloat16 [8, 8, 128], P(None, 'head'), may hold values from -6 to 6
- lengths: int32 [8], replicated, may hold values from 1024 to 4096, as said below
- out_weight: bfloat16 [5120, 5120], P('head', 'seq'), may hold values from -0.078125 to 0.078125
Outputs:
- projected: float32 [8, 5120], P(None, 'seq')
Inputs may be any that keep to these rules, and one draw needn't show every extreme that they name: `lengths`: some sequence has exactly 4096 cached tokens.
All inputs are finite; a program needn't handle non-finite values.
Results may differ from a plain program's by a relative error of at most 0.0064.
Values sent between devices are 32-bit elements; how exact they have to be, the bound alone decides.
No kernel may reach another device: no remote copies, remote signals or barrier semaphores. Data moves between devices by JAX's collectives and lax.ppermute only.
A program may use at most 64 MiB of HBM per device.

v0:
```python
import math
import jax
import jax.numpy as jnp
from jax import lax
from jax.sharding import PartitionSpec as P

THETA_BASE = 10000000.0
NEG_FILL = -1e30


def apply_rotary(values, positions):
    half_width = values.shape[-1] // 2
    frequency = jnp.exp(
        jnp.arange(half_width, dtype=jnp.float32)
        * jnp.float32(-2.0 * math.log(THETA_BASE) / values.shape[-1])
    )
    angles = positions[..., None] * frequency
    cos_part = jnp.cos(angles)
    sin_part = jnp.sin(angles)
    lower_section = values[..., :half_width]
    upper_half = values[..., half_width:]
    return jnp.concatenate(
        [
            lower_section * cos_part - upper_half * sin_part,
            upper_half * cos_part + lower_section * sin_part,
        ],
        axis=-1,
    )


def query_positions(lengths, stretch_len):
    remainder = lengths % stretch_len
    return jnp.stack(
        [
            remainder,
            remainder + stretch_len,
            jnp.zeros_like(remainder) + (stretch_len + stretch_len // 2),
        ],
        axis=-1,
    ).astype(jnp.float32)


def body(query, key_cache, value_cache, new_key, new_value, lengths, out_weight):
    seq_count = lax.axis_size("seq")
    batch, span_len, kv_local, head_width = key_cache.shape
    heads_local = query.shape[1]
    group_size = heads_local // kv_local
    stretch_len = span_len * seq_count // 8
    scaling = 1.0 / math.sqrt(head_width)
    positions = lax.axis_index("seq") * span_len + jnp.arange(span_len, dtype=jnp.int32)
    query_pos = query_positions(lengths, stretch_len)
    query_rot = apply_rotary(query.astype(jnp.float32)[:, None], query_pos[:, :, None]).astype(
        jnp.bfloat16
    )
    key_rot = apply_rotary(
        key_cache.astype(jnp.float32), (positions % stretch_len).astype(jnp.float32)[None, :, None]
    ).astype(jnp.bfloat16)
    query_by_group = query_rot.reshape(batch, 3, kv_local, group_size, head_width)
    query_stretch = lengths // stretch_len
    key_stretch = positions // stretch_len
    key_class = jnp.where(
        key_stretch[None] == query_stretch[:, None],
        0,
        jnp.where(key_stretch[None] == query_stretch[:, None] - 1, 1, 2),
    )
    block_class = key_class[:, 0][:, None, None, None]
    picked = jnp.where(
        block_class == 0,
        query_by_group[:, 0],
        jnp.where(block_class == 1, query_by_group[:, 1], query_by_group[:, 2]),
    )
    selected_branch = (
        jnp.einsum("bkgd,bpkd->bkgp", picked, key_rot, preferred_element_type=jnp.float32) * scaling
    )
    live_mask = (positions[None] < lengths[:, None])[:, None, None, :]
    masked = jnp.where(live_mask, selected_branch, NEG_FILL)
    block_max = jnp.max(masked, axis=-1)
    weights = jnp.where(live_mask, jnp.exp(masked - block_max[..., None]), 0.0)
    block_total = jnp.sum(weights, axis=-1)
    block_acc = jnp.einsum(
        "bkgp,bpkd->bkgd",
        weights.astype(jnp.bfloat16),
        value_cache,
        preferred_element_type=jnp.float32,
    )
    current_key = apply_rotary(new_key.astype(jnp.float32), query_pos[:, 0][:, None]).astype(
        jnp.bfloat16
    )
    self_score = (
        jnp.einsum(
            "lmzu,lmu->lmz", query_by_group[:, 0], current_key, preferred_element_type=jnp.float32
        )
        * scaling
    )
    fresh_values = new_value.astype(jnp.float32)[:, :, None, :]
    top_score = lax.pmax(jnp.maximum(block_max, self_score), "seq")
    factor = jnp.exp(block_max - top_score)
    summed_total, summed_acc = lax.psum(
        (block_total * factor, block_acc * factor[..., None]), "seq"
    )
    self_factor = jnp.exp(self_score - top_score)
    total = summed_total + self_factor
    accum = summed_acc + fresh_values * self_factor[..., None]
    attended = (
        (accum / total[..., None]).reshape(batch, heads_local * head_width).astype(jnp.bfloat16)
    )
    partial_value = jnp.dot(attended, out_weight, preferred_element_type=jnp.float32)
    return lax.psum(partial_value, "head")


def solution(mesh):
    placed = (
        P(None, "head", None),
        P(None, "seq", "head", None),
        P(None, "seq", "head", None),
        P(None, "head", None),
        P(None, "head", None),
        P(),
        P("head", "seq"),
    )
    return jax.shard_map(
        body, mesh=mesh, in_specs=placed, out_specs=P(None, "seq"), check_vma=False
    )
```

profile of v0, /device:TPU:0, one launch (start us, length us, event | category | flops | bytes accessed | tf_op | source)
XLA Modules:
  0.0 84.6 jit_solution(15212608247679977557)
XLA Ops:
  0.0 0.0 copy-start
  0.0 4.1 %copy_convert_fusion = f32[8,512,2,128]{3,1,2,0:T(8,128)} fusion(bf16[8,512,2,128]{3,2,1,0:T(2,128)(2,1)} %param.8), kind=kLoop, calls=%fused_computation.8 | loop fusion | flops 1048576 | bytes 6291456 | tf_op jit(solution)/shard_map/convert_element_type | solution.py:56
  4.1 1.0 %multiply_cosine_fusion = (f32[512,64]{1,0:T(8,128)S(1)}, f32[512,64]{1,0:T(8,128)S(1)}) fusion(f32[64]{0:T(128)S(1)} %multiply_exponential_fusion, f32[512]{0:T(512)S(1)} %get-tuple-element.35), kind=kLoop, calls=%fused_computation.13 | loop fusion | flops 32768 | bytes 264448 | tf_op jit(solution)/shard_map/cos | solution.py:18
  5.1 0.0 copy-start.4
  5.1 0.0 copy-start.1
  5.1 4.9 %subtract_convert_fusion = (bf16[8,512,2,64]{3,1,2,0:T(8,128)(2,1)S(1)}, bf16[8,512,2,64]{3,1,2,0:T(8,128)(2,1)S(1)}) fusion(f32[8,512,2,128]{3,1,2,0:T(8,128)} %copy_convert_fusion, f32[512,64]{1,0:T(8,128)S(1)} %get-tuple-element.27, f32[512,64]{1,0:T(8,128)S(1)} %get-tuple-element.26), kind=kLoop, calls=%fused_computation.1 | loop fusion | flops 4194304 | bytes 6553600 | tf_op jit(solution)/shard_map/convert.3
  10.1 0.0 copy-done.4
  10.1 0.1 pad.8.clone
  10.2 0.1 add_convert_fusion.3
  10.3 0.1 multiply_cosine_fusion.1
  10.4 0.0 copy-done.1
  10.4 0.1 fusion.46
  10.5 0.1 add_convert_fusion.1
  10.6 0.5 slice.45
  11.1 0.7 compare_bitcast_fusion.1
  11.8 0.1 broadcast_compare_fusion
  11.9 0.0 copy-start.2
  11.9 1.4 %fusion.47 = (f32[8,2,5]{2,1,0:T(2,128)S(1)}, f32[8,2,5,512]{3,2,1,0:T(8,128)S(1)}) fusion(bf16[8,512,2,64]{3,1,2,0:T(8,128)(2,1)S(1)} %get-tuple-element.17, bf16[8,512,2,64]{3,1,2,0:T(8,128)(2,1)S(1)} %get-tuple-element.16, bf16[8,3,2,5,64]{4,3,2,0,1:T(8,128)(2,1)S(1)} %get-tuple-element.19, bf16[8,3,2,5,64]{4,3,2,0,1:T(8,128)(2,1)S(1)} %get-tuple-element.18, ...), kind=kOutput, calls=%fused_computation.83 | convolution fusion | flops 14946224 | bytes 2326864 | tf_op jit(solution)/shard_map/bkgd,bpkd->bkgp/dot_general | solution.py:73
  13.3 0.0 copy-start.3
  13.3 0.2 fusion.15
  13.5 0.0 copy-done.2
  13.5 0.1 multiply_cosine_fusion.2
  13.6 0.1 subtract_convert_fusion.2
  13.7 0.1 maximum_bitcast_fusion
  13.8 0.2 fusion.33
  14.0 23.4 %pmax.7 = f32[8,2,5]{2,1,0:T(2,128)S(1)} all-reduce(f32[8,2,5]{2,1,0:T(2,128)S(1)} %multiply_maximum_fusion), channel_id=1, replica_groups=mesh['seq'=8,'head'=4] {'seq'}, use_global_device_ids=true, to_apply=%region_1.2 | all-reduce | flops 80 | bytes 640 | tf_op jit(solution)/shard_map/pmax | solution.py:96
  37.5 0.0 copy-done
  37.5 0.4 fusion.12
  37.9 33.9 %all-reduce = (f32[8,2,5,128]{3,2,1,0:T(8,128)S(1)}, f32[8,2,5]{2,1,0:T(2,128)S(1)}) all-reduce(f32[8,2,5,128]{3,2,1,0:T(8,128)S(1)} %fusion.12, f32[8,2,5]{2,1,0:T(2,128)S(1)} %bitcast.58), channel_id=1, replica_groups=mesh['seq'=8,'head'=4] {'seq'}, use_global_device_ids=true, to_apply=%region_2.3 | all-reduce | flops 10320 | bytes 82560 | tf_op jit(solution)/shard_map/psum | solution.py:98
  71.9 0.0 copy-done.3
  71.9 0.1 divide_convert_fusion
  72.0 1.8 %fusion.48 = f32[8,640]{1,0:T(8,128)S(1)} fusion(bf16[8,1280]{1,0:T(8,128)(2,1)S(1)} %convert_element_type.44, bf16[1280,640]{1,0:T(8,128)(2,1)} %param.13), kind=kOutput, calls=%fused_computation.84 | convolution fusion | flops 13107200 | bytes 1679360 | tf_op jit(solution)/shard_map/dot_general | solution.py:107
  73.8 10.9 %psum.23 = f32[8,640]{1,0:T(8,128)} all-reduce(f32[8,640]{1,0:T(8,128)S(1)} %fusion.48), channel_id=1, replica_groups=mesh['seq'=8,'head'=4] {'head'}, use_global_device_ids=true, to_apply=%region_5.6 | all-reduce | flops 5120 | bytes 40960 | tf_op jit(solution)/shard_map/psum | solution.py:108
  (16 shorter events, 0.2 us)
Async XLA Ops:
  0.0 37.5 %copy-start = (bf16[8,512,2,128]{3,2,1,0:T(2,128)(2,1)S(1)}, bf16[8,512,2,128]{3,2,1,0:T(2,128)(2,1)}, u32[]{:S(2)}) copy-start(bf16[8,512,2,128]{3,2,1,0:T(2,128)(2,1)} %param.9) | copy-start | bytes 6291460
  5.1 5.0 %copy-start.4 = (s32[8]{0:T(128)S(1)}, s32[8]{0:T(128)}, u32[]{:S(2)}) copy-start(s32[8]{0:T(128)} %param.12) | copy-start | bytes 100
  5.1 5.3 %copy-start.1 = (bf16[8,10,128]{2,0,1:T(8,128)(2,1)S(1)}, bf16[8,10,128]{2,0,1:T(8,128)(2,1)}, u32[]{:S(2)}) copy-start(bf16[8,10,128]{2,0,1:T(8,128)(2,1)} %param.7) | copy-start | bytes 61444
  11.9 1.6 %copy-start.2 = (bf16[8,2,128]{2,1,0:T(2,128)(2,1)S(1)}, bf16[8,2,128]{2,1,0:T(2,128)(2,1)}, u32[]{:S(2)}) copy-start(bf16[8,2,128]{2,1,0:T(2,128)(2,1)} %param.10) | copy-start | bytes 12292
  13.3 58.6 %copy-start.3 = (bf16[8,2,128]{2,1,0:T(2,128)(2,1)S(1)}, bf16[8,2,128]{2,1,0:T(2,128)(2,1)}, u32[]{:S(2)}) copy-start(bf16[8,2,128]{2,1,0:T(2,128)(2,1)} %param.11) | copy-start | bytes 12292
where the time goes:
time: 84.9 us; the launch traced here: 84.6 us
  blocking collectives  68.2 us (80%)
  other arithmetic  11.7 us (14%)
  matrix products  3.78 us (4%)
    psum x1, blocking collectives, body(): lax.psum((block_total * factor, block_acc * factor[..., None]), 'seq')  33.9 us
    pmax x1, blocking collectives, body(): top_score = lax.pmax(jnp.maximum(block_max, self_score), 'seq')  23.4 us
    psum x1, blocking collectives, body(): return lax.psum(partial_value, 'head')  10.9 us
    another operation x3, other arithmetic  5.08 us
    convert_element_type x1, other arithmetic, body(): key_cache.astype(jnp.float32)  4.08 us
    dot_general x1, matrix products, body(): jnp.dot(attended, out_weight, preferred_element_type=jnp.float32)  1.75 us

commit v1 on v0

--- a/solution.py
+++ b/solution.py
@@ -6,6 +6,11 @@
 
 THETA_BASE = 10000000.0
 NEG_FILL = -1e30
+
+
+def take_the_gates(page):
+    earlier = jnp.sum(lax.all_gather(page, "head"), axis=0)
+    return earlier
 
 
 def apply_rotary(values, positions):
@@ -105,7 +110,7 @@
         (accum / total[..., None]).reshape(batch, heads_local * head_width).astype(jnp.bfloat16)
     )
     partial_value = jnp.dot(attended, out_weight, preferred_element_type=jnp.float32)
-    return lax.psum(partial_value, "head")
+    return take_the_gates(partial_value)
 
 
 def solution(mesh):

time: 84.9 us -> 79.9 us (0.941)
  blocking collectives: 68.2 us -> 62.6 us
    psum x1 -> x0, blocking collectives: 10.9 us -> none  [body(): return lax.psum(partial_value, 'head')]
    all_gather x0 -> x1, blocking collectives: none -> 5.28 us  [take_the_gates(): earlier = jnp.sum(lax.all_gather(page, 'head'), axis=0)]
where the time goes in v1:
time: 79.9 us; the launch traced here: 79.7 us
  blocking collectives  62.6 us (78%)
  other arithmetic  12.3 us (15%)
  matrix products  3.78 us (5%)
    psum x1, blocking collectives, body(): lax.psum((block_total * factor, block_acc * factor[..., None]), 'seq')  33.9 us
    pmax x1, blocking collectives, body(): top_score = lax.pmax(jnp.maximum(block_max, self_score), 'seq')  23.4 us
    all_gather x1, blocking collectives, take_the_gates(): earlier = jnp.sum(lax.all_gather(page, 'head'), axis=0)  5.28 us
    another operation x3, other arithmetic  5.08 us
    convert_element_type x1, other arithmetic, body(): key_cache.astype(jnp.float32)  4.08 us
    dot_general x1, matrix products, body(): jnp.dot(attended, out_weight, preferred_element_type=jnp.float32)  1.75 us

profile of v1, /device:TPU:0, one launch (start us, length us, event | category | flops | bytes accessed | tf_op | source)
XLA Modules:
  0.0 79.7 jit_solution(10005468552995350053)
XLA Ops:
  0.0 0.0 copy-start
  0.0 4.1 %copy_convert_fusion = f32[8,512,2,128]{3,1,2,0:T(8,128)} fusion(bf16[8,512,2,128]{3,2,1,0:T(2,128)(2,1)} %param.8), kind=kLoop, calls=%fused_computation.8 | loop fusion | flops 1048576 | bytes 6291456 | tf_op jit(solution)/shard_map/convert_element_type | solution.py:61
  4.1 1.0 %multiply_cosine_fusion = (f32[512,64]{1,0:T(8,128)S(1)}, f32[512,64]{1,0:T(8,128)S(1)}) fusion(f32[64]{0:T(128)S(1)} %multiply_exponential_fusion, f32[512]{0:T(512)S(1)} %get-tuple-element.35), kind=kLoop, calls=%fused_computation.13 | loop fusion | flops 32768 | bytes 264448 | tf_op jit(solution)/shard_map/cos | solution.py:23
  5.1 0.0 copy-start.4
  5.1 0.0 copy-start.1
  5.1 4.9 %subtract_convert_fusion = (bf16[8,512,2,64]{3,1,2,0:T(8,128)(2,1)S(1)}, bf16[8,512,2,64]{3,1,2,0:T(8,128)(2,1)S(1)}) fusion(f32[8,512,2,128]{3,1,2,0:T(8,128)} %copy_convert_fusion, f32[512,64]{1,0:T(8,128)S(1)} %get-tuple-element.27, f32[512,64]{1,0:T(8,128)S(1)} %get-tuple-element.26), kind=kLoop, calls=%fused_computation.1 | loop fusion | flops 4194304 | bytes 6553600 | tf_op jit(solution)/shard_map/convert.3
  10.1 0.0 copy-done.4
  10.1 0.1 pad.8.clone
  10.2 0.1 add_convert_fusion.3
  10.3 0.1 multiply_cosine_fusion.1
  10.4 0.0 copy-done.1
  10.4 0.1 fusion.46
  10.5 0.1 add_convert_fusion.1
  10.6 0.5 slice.45
  11.1 0.7 compare_bitcast_fusion.1
  11.8 0.1 broadcast_compare_fusion
  11.9 0.0 copy-start.2
  11.9 1.4 %fusion.47 = (f32[8,2,5]{2,1,0:T(2,128)S(1)}, f32[8,2,5,512]{3,2,1,0:T(8,128)S(1)}) fusion(bf16[8,512,2,64]{3,1,2,0:T(8,128)(2,1)S(1)} %get-tuple-element.17, bf16[8,512,2,64]{3,1,2,0:T(8,128)(2,1)S(1)} %get-tuple-element.16, bf16[8,3,2,5,64]{4,3,2,0,1:T(8,128)(2,1)S(1)} %get-tuple-element.19, bf16[8,3,2,5,64]{4,3,2,0,1:T(8,128)(2,1)S(1)} %get-tuple-element.18, ...), kind=kOutput, calls=%fused_computation.84 | convolution fusion | flops 14946224 | bytes 2326864 | tf_op jit(solution)/shard_map/bkgd,bpkd->bkgp/dot_general | solution.py:78
  13.3 0.0 copy-start.3
  13.3 0.2 fusion.15
  13.5 0.0 copy-done.2
  13.5 0.1 multiply_cosine_fusion.2
  13.6 0.1 subtract_convert_fusion.2
  13.7 0.1 maximum_bitcast_fusion
  13.8 0.2 fusion.33
  14.0 23.4 %pmax.7 = f32[8,2,5]{2,1,0:T(2,128)S(1)} all-reduce(f32[8,2,5]{2,1,0:T(2,128)S(1)} %multiply_maximum_fusion), channel_id=1, replica_groups=mesh['seq'=8,'head'=4] {'seq'}, use_global_device_ids=true, to_apply=%region_1.2 | all-reduce | flops 80 | bytes 640 | tf_op jit(solution)/shard_map/pmax | solution.py:101
  37.5 0.0 copy-done
  37.5 0.4 fusion.12
  37.9 33.9 %all-reduce = (f32[8,2,5,128]{3,2,1,0:T(8,128)S(1)}, f32[8,2,5]{2,1,0:T(2,128)S(1)}) all-reduce(f32[8,2,5,128]{3,2,1,0:T(8,128)S(1)} %fusion.12, f32[8,2,5]{2,1,0:T(2,128)S(1)} %bitcast.60), channel_id=1, replica_groups=mesh['seq'=8,'head'=4] {'seq'}, use_global_device_ids=true, to_apply=%region_2.3 | all-reduce | flops 10320 | bytes 82560 | tf_op jit(solution)/shard_map/psum | solution.py:103
  71.9 0.0 copy-done.3
  71.9 0.1 divide_convert_fusion
  72.0 1.8 %fusion.48 = f32[8,640]{1,0:T(8,128)S(1)} fusion(bf16[8,1280]{1,0:T(8,128)(2,1)S(1)} %convert_element_type.44, bf16[1280,640]{1,0:T(8,128)(2,1)} %param.13), kind=kOutput, calls=%fused_computation.85 | convolution fusion | flops 13107200 | bytes 1679360 | tf_op jit(solution)/shard_map/dot_general | solution.py:112
  73.8 5.3 %all-gather = f32[32,640]{1,0:T(8,128)S(1)} all-gather(f32[8,640]{1,0:T(8,128)S(1)} %fusion.48), channel_id=2, replica_groups=mesh['seq'=8,'head'=4] {'head'}, dimensions={0}, use_global_device_ids=true | all-gather | bytes 102400 | tf_op jit(solution)/shard_map/all_gather | solution.py:12
  79.1 0.6 bitcast_reduce_fusion
  (16 shorter events, 0.2 us)
Async XLA Ops:
  0.0 37.5 %copy-start = (bf16[8,512,2,128]{3,2,1,0:T(2,128)(2,1)S(1)}, bf16[8,512,2,128]{3,2,1,0:T(2,128)(2,1)}, u32[]{:S(2)}) copy-start(bf16[8,512,2,128]{3,2,1,0:T(2,128)(2,1)} %param.9) | copy-start | bytes 6291460
  5.1 5.0 %copy-start.4 = (s32[8]{0:T(128)S(1)}, s32[8]{0:T(128)}, u32[]{:S(2)}) copy-start(s32[8]{0:T(128)} %param.12) | copy-start | bytes 100
  5.1 5.3 %copy-start.1 = (bf16[8,10,128]{2,0,1:T(8,128)(2,1)S(1)}, bf16[8,10,128]{2,0,1:T(8,128)(2,1)}, u32[]{:S(2)}) copy-start(bf16[8,10,128]{2,0,1:T(8,128)(2,1)} %param.7) | copy-start | bytes 61444
  11.9 1.6 %copy-start.2 = (bf16[8,2,128]{2,1,0:T(2,128)(2,1)S(1)}, bf16[8,2,128]{2,1,0:T(2,128)(2,1)}, u32[]{:S(2)}) copy-start(bf16[8,2,128]{2,1,0:T(2,128)(2,1)} %param.10) | copy-start | bytes 12292
  13.3 58.6 %copy-start.3 = (bf16[8,2,128]{2,1,0:T(2,128)(2,1)S(1)}, bf16[8,2,128]{2,1,0:T(2,128)(2,1)}, u32[]{:S(2)}) copy-start(bf16[8,2,128]{2,1,0:T(2,128)(2,1)} %param.11) | copy-start | bytes 12292
